TPU v7x, 32 devices: a whole 2x2x4 slice. The times are simulated.
32 devices in a mesh: expert: 8 (over y, x, core), dp: 4 (over z).
Axes of the slice: x: 2, y: 2, z: 4, core: 2. Of those that a mesh axis runs over, the one named last changes fastest.
Arguments:
- gradient: bfloat16 [4, 1, 14336, 2048], P('dp', None, None, 'expert'), may hold values from -6 to 6
- momentum: float32 [4, 1, 14336, 2048], P('dp', None, 'expert'), may hold values from -6 to 6
- group_index: int32 [224, 32, 4, 32], P('expert'), may hold values from 0 to 4095, all different within a row
Outputs:
- momentum_next: float32 [4, 1, 14336, 2048], P('dp', None, 'expert')
- update: float32 [1, 14336, 2048], P(None, None, 'expert')
Inputs may be any that keep to these rules, and one draw needn't show every extreme that they name: `group_index`: an entry names the coefficient at row frequency (entry // 64) and column frequency (entry % 64) of its block; the 32 entries of one block and replica differ.
All inputs are finite; a program needn't handle non-finite values.
Results may differ from a plain program's by a relative error of at most 0.0003.
Values may be sent and summed in bfloat16 or wider, within the bound.
No kernel may reach another device: no remote copies, remote signals or barrier semaphores. Data moves between devices by JAX's collectives and lax.ppermute only.
A program may use at most 192 MiB of HBM per device.

v0:
```python
import math
import jax
import jax.numpy as jnp
from jax import lax
from jax.sharding import PartitionSpec as P

SPAN = 64
MOMENTUM_DECAY = 0.999
HIGHEST_PRECISION = lax.Precision.HIGHEST


def cosine_table(order_size):
    frequency = jnp.arange(order_size, dtype=jnp.float32)[:, None]
    position = jnp.arange(order_size, dtype=jnp.float32)[None, :]
    weighting = jnp.where(frequency == 0, math.sqrt(1.0 / order_size), math.sqrt(2.0 / order_size))
    return weighting * jnp.cos(math.pi * (2.0 * position + 1.0) * frequency / (2.0 * order_size))


def forward(blocks, cosine):
    return jnp.einsum("ui,piqj,vj->pquv", cosine, blocks, cosine, precision=HIGHEST_PRECISION)


def inverse(coeffs, cosine):
    return jnp.einsum("ui,pquv,vj->piqj", cosine, coeffs, cosine, precision=HIGHEST_PRECISION)


def place(values, picked, total):
    count_rows = picked.shape[0]
    count_cols = picked.shape[1]
    row_ids = jnp.arange(count_rows, dtype=jnp.int32)[:, None, None]
    col_ids = jnp.arange(count_cols, dtype=jnp.int32)[None, :, None]
    empty = jnp.zeros((count_rows, count_cols, total), jnp.float32)
    return empty.at[row_ids, col_ids, picked].add(values)


def on_device(gradient, momentum, group_index):
    cosine = cosine_table(SPAN)
    replica = lax.axis_index("dp")
    shifted = lax.all_to_all(gradient, "expert", split_axis=2, concat_axis=3, tiled=True)
    row_count = shifted.shape[1] * shifted.shape[2]
    col_count = shifted.shape[3]
    decayed = MOMENTUM_DECAY * momentum.reshape(row_count, col_count) + shifted.reshape(
        row_count, col_count
    ).astype(jnp.float32)
    block_rows = row_count // SPAN
    block_cols = col_count // SPAN
    blocks = decayed.reshape(block_rows, SPAN, block_cols, SPAN)
    coeffs = forward(blocks, cosine).reshape(block_rows, block_cols, SPAN * SPAN)
    own = lax.dynamic_index_in_dim(group_index, replica, 2, keepdims=False)
    values = jnp.take_along_axis(coeffs, own, axis=2)
    selected = place(values, own, SPAN * SPAN).reshape(block_rows, block_cols, SPAN, SPAN)
    restored = inverse(selected, cosine).reshape(row_count, col_count)
    momentum_next = (decayed - restored).reshape(momentum.shape)
    total = lax.psum(restored, "dp")
    update = lax.all_to_all(total[None], "expert", split_axis=2, concat_axis=1, tiled=True)
    return (momentum_next, update)


def solution(mesh):
    placed = (
        P("dp", None, None, "expert"),
        P("dp", None, "expert", None),
        P("expert", None, None, None),
    )
    return jax.shard_map(
        on_device,
        mesh=mesh,
        in_specs=placed,
        out_specs=(P("dp", None, "expert", None), P(None, None, "expert")),
        check_vma=False,
    )
```

profile of v0, /device:TPU:0, one launch (start us, length us, event | category | flops | bytes accessed | tf_op | source)
XLA Modules:
  0.0 1791.6 jit_solution(7726705985942069426)
XLA Ops:
  21.6 74.4 %reduce.4 = bf16[14336,256]{1,0:T(8,128)(2,1)} reduce(bf16[14336,1,1,256]{3,2,1,0:T(2,128)(2,1)} %bitcast.50, bf16[]{:T(256)} %broadcast.103), dimensions={1,2}, to_apply=%bitcast.46.reduce_sub_computation | reduce | bytes 14680066
  113.9 14.1 broadcast_multiply_fusion
  128.0 24.3 %mul.98 = f32[28,64,32,64]{3,2,1,0:T(8,128)} reshape(f32[1,1,1792,2048]{3,2,1,0:T(8,128)} %broadcast_multiply_fusion) | data formatting | bytes 29360128 | tf_op jit(solution)/shard_map/mul | solution.py:42
  152.5 40.9 %all-to-all-done = bf16[8,2,229376]{2,1,0:T(2,128)(2,1)} async-done(((bf16[8,2,229376]{2,1,0:T(2,128)(2,1)}), bf16[8,2,229376]{2,1,0:T(2,128)(2,1)}, u32[]{:S(2)}, u32[]{:S(2)}) %all-to-all-start) | async-done | bytes 7340064 | tf_op jit(solution)/shard_map/all_to_all | solution.py:39
  205.5 15.9 copy.46
  221.4 21.6 %reshape.112 = f32[28,64,32,64]{3,2,1,0:T(8,128)} reshape(f32[1,1,1792,8,256]{4,3,2,1,0:T(8,128)} %bitcast.47) | data formatting | bytes 29360128 | tf_op jit(solution)/shard_map/convert_element_type | solution.py:44
  243.1 29.9 %add.64 = f32[28,64,32,64]{3,2,1,0:T(8,128)} add(f32[28,64,32,64]{3,2,1,0:T(8,128)} %mul.98, f32[28,64,32,64]{3,2,1,0:T(8,128)} %reshape.112) | non-fusion elementwise | flops 3670016 | bytes 44040192 | tf_op jit(solution)/shard_map/add | solution.py:42
  273.0 52.6 %fusion = f32[28,32,64,64]{2,3,1,0:T(8,128)} fusion(f32[28,64,32,64]{3,2,1,0:T(8,128)} %add.64, f32[64]{0:T(128)S(1)} %get-tuple-element.5, f32[64]{0:T(128)S(1)} %get-tuple-element.4), kind=kOutput, calls=%fused_computation.2 | convolution fusion | flops 2818584576 | bytes 29360640 | tf_op jit(solution)/shard_map/ui,piqj,vj->pquv/dot_general | solution.py:20
  325.6 29.6 %fusion.7 = f32[28,32,64,64]{3,2,1,0:T(8,128)} fusion(f32[28,32,64,64]{2,3,1,0:T(8,128)} %fusion, f32[64]{0:T(128)S(1)} %get-tuple-element.5, f32[64]{0:T(128)S(1)} %get-tuple-element.4), kind=kOutput, calls=%fused_computation.21 | convolution fusion | flops 2818584576 | bytes 29360640 | tf_op jit(solution)/shard_map/ui,piqj,vj->pquv/dot_general | solution.py:20
  355.3 24.7 %reshape.101 = f32[28,32,4096]{2,1,0:T(8,128)} reshape(f32[28,32,64,64]{3,2,1,0:T(8,128)} %fusion.7) | data formatting | bytes 29360128 | tf_op jit(solution)/shard_map/reshape | solution.py:48
  380.0 398.1 %gather_fusion = f32[28672]{0:T(1024)S(1)} fusion(f32[28,32,4096]{2,1,0:T(8,128)} %reshape.101, s32[28672]{0:T(1024)S(1)} %reshape.115), kind=kCustom, calls=%fused_computation | custom fusion | bytes 573440 | tf_op jit(solution)/shard_map/jit(take_along_axis)/gather | solution.py:50
  778.6 156.3 %scatter_custom_fusion = f32[3670016]{0:T(1024)} fusion(s32[28672]{0:T(1024)} %reshape.121, f32[28672]{0:T(1024)S(1)} %reshape.123, f32[]{:T(128)} %constant.15.clone.1), kind=kCustom, calls=%fused_computation.7 | custom fusion | flops 28672 | bytes 14680576
  934.9 22.2 %reshape.102 = f32[28,32,64,64]{3,2,1,0:T(8,128)} reshape(f32[3670016]{0:T(1024)} %scatter_custom_fusion) | data formatting | bytes 29360128 | tf_op jit(solution)/shard_map/reshape | solution.py:51
  957.1 34.3 %fusion.5 = f32[28,32,64,64]{2,3,1,0:T(8,128)} fusion(f32[28,32,64,64]{3,2,1,0:T(8,128)} %reshape.102, f32[64]{0:T(128)S(1)} %copy-done.7, f32[64]{0:T(128)S(1)} %copy-done.5), kind=kOutput, calls=%fused_computation.19 | convolution fusion | flops 2818584576 | bytes 29360640 | tf_op jit(solution)/shard_map/ui,pquv,vj->piqj/dot_general | solution.py:24
  991.3 29.2 %convolution_bitcast_fusion = f32[28,64,32,64]{3,1,2,0:T(8,128)S(1)} fusion(f32[28,32,64,64]{2,3,1,0:T(8,128)} %fusion.5, f32[64]{0:T(128)S(1)} %copy-done.7, f32[64]{0:T(128)S(1)} %copy-done.5), kind=kOutput, calls=%fused_computation.6 | convolution fusion | flops 2818584576 | bytes 29360640 | tf_op jit(solution)/shard_map/ui,pquv,vj->piqj/dot_general | solution.py:24
  1020.6 19.3 %copy.33 = f32[28,64,32,64]{3,2,1,0:T(8,128)} copy(f32[28,64,32,64]{3,1,2,0:T(8,128)S(1)} %convolution_bitcast_fusion) | data formatting | bytes 29360128 | tf_op jit(solution)/shard_map/ui,pquv,vj->piqj/transpose | solution.py:24
  1039.9 25.4 %broadcast_in_dim.39 = f32[1,1792,2048]{2,1,0:T(8,128)} reshape(f32[28,64,32,64]{3,2,1,0:T(8,128)} %copy.33) | data formatting | bytes 29360128 | tf_op jit(solution)/shard_map/broadcast_in_dim | solution.py:55
  1065.3 494.5 %all-reduce.2.cloned.1.call-done = f32[1,1792,2048]{2,1,0:T(8,128)} async-done(((f32[1,1792,2048]{2,1,0:T(8,128)}), f32[1,1792,2048]{2,1,0:T(8,128)}) %all-reduce.2.cloned.1.call-update) | async-done | bytes 14680080 | tf_op jit(solution)/shard_map/psum | solution.py:54
  1559.7 32.1 %copy.35 = f32[1,1792,2048]{1,0,2:T(1,128)} copy(f32[1,1792,2048]{2,1,0:T(8,128)} %all-reduce.2.cloned.1.call-done) | data formatting | bytes 29360128 | tf_op jit(solution)/shard_map/psum | solution.py:54
  1597.4 25.4 %reshape.103 = f32[1,1,1792,2048]{3,2,1,0:T(8,128)} reshape(f32[28,64,32,64]{3,2,1,0:T(8,128)} %copy.33) | data formatting | bytes 29360128 | tf_op jit(solution)/shard_map/reshape | solution.py:52
  1622.8 15.8 reshape.111
  1638.6 20.9 %add_subtract_fusion = f32[1,1,1792,2048]{3,2,1,0:T(8,128)} fusion(f32[1,1,1792,2048]{3,2,1,0:T(8,128)} %reshape.103, f32[1,1,1792,2048]{3,2,1,0:T(8,128)} %reshape.111, f32[1,1,1792,2048]{3,2,1,0:T(8,128)} %param.4), kind=kLoop, calls=%fused_computation.5 | loop fusion | flops 11010048 | bytes 58720256 | tf_op jit(solution)/shard_map/sub | solution.py:53
  1659.6 99.3 %all-to-all-done.1 = f32[1,1792,2048]{1,0,2:T(1,128)} async-done(((f32[1,1792,2048]{1,0,2:T(1,128)}), f32[1,1792,2048]{1,0,2:T(1,128)}, u32[]{:S(2)}, u32[]{:S(2)}) %all-to-all-start.1) | async-done | bytes 14680096 | tf_op jit(solution)/shard_map/all_to_all | solution.py:55
  1770.2 14.4 copy.36
  (42 shorter events, 61.9 us)
Async XLA Ops:
  7.2 103.7 %copy-start = (s32[28,32,4,32]{3,2,1,0:T(4,128)S(1)}, s32[28,32,4,32]{3,2,1,0:T(4,128)}, u32[]{:S(2)}) copy-start(s32[28,32,4,32]{3,2,1,0:T(4,128)} %param.5) | copy-start | bytes 1376260
  96.0 16.4 copy-start.9
  96.0 16.6 copy-start.8
  105.1 88.4 %all-to-all-start = ((bf16[8,2,229376]{2,1,0:T(2,128)(2,1)}), bf16[8,2,229376]{2,1,0:T(2,128)(2,1)}, u32[]{:S(2)}, u32[]{:S(2)}) async-start(bf16[8,2,229376]{2,1,0:T(2,128)(2,1)} %reshape.130), calls=%async_computation | async-start | bytes 14680064 | tf_op jit(solution)/shard_map/all_to_all | solution.py:39
  110.3 1449.5 %all-reduce.2.cloned.1.call-start = ((), (), s32[]{:S(2)}) async-start(), calls=%async_computation.2 | async-start | bytes 29360128 | tf_op jit(solution)/shard_map/psum | solution.py:54
  111.3 0.8 copy-start.2
  152.5 173.1 %copy-start.4 = (f32[64]{0:T(128)}, f32[64]{0:T(128)S(1)}, u32[]{:S(2)}) copy-start(f32[64]{0:T(128)S(1)} %get-tuple-element.4) | copy-start | bytes 772
  152.5 173.1 %copy-start.6 = (f32[64]{0:T(128)}, f32[64]{0:T(128)S(1)}, u32[]{:S(2)}) copy-start(f32[64]{0:T(128)S(1)} %get-tuple-element.5) | copy-start | bytes 772
  380.0 398.3 %copy-start.3 = (s32[28,32,1,32]{3,2,1,0:T(1,128)S(1)}, s32[28,32,1,32]{3,2,1,0:T(1,128)}, u32[]{:S(2)}) copy-start(s32[28,32,1,32]{3,2,1,0:T(1,128)} %copy-done.2) | copy-start | bytes 344068
  934.9 22.2 %copy-start.5 = (f32[64]{0:T(128)S(1)}, f32[64]{0:T(128)}, u32[]{:S(2)}) copy-start(f32[64]{0:T(128)} %copy-done.4) | copy-start | bytes 772
  934.9 22.2 %copy-start.7 = (f32[64]{0:T(128)S(1)}, f32[64]{0:T(128)}, u32[]{:S(2)}) copy-start(f32[64]{0:T(128)} %copy-done.6) | copy-start | bytes 772
  1591.8 167.0 %all-to-all-start.1 = ((f32[1,1792,2048]{1,0,2:T(1,128)}), f32[1,1792,2048]{1,0,2:T(1,128)}, u32[]{:S(2)}, u32[]{:S(2)}) async-start(f32[1,1792,2048]{1,0,2:T(1,128)} %copy.35), calls=%async_computation.1 | async-start | bytes 29360128 | tf_op jit(solution)/shard_map/all_to_all | solution.py:55
  1770.2 14.4 copy-start.1
Sparse Core Ops, SparseCore 0:
  1065.4 494.3 all-reduce.1
where the time goes:
time: 1810 us; the launch traced here: 1790 us
  local copies, waits for them, and re-layouts  689 us (38%)
  waiting for transfers between devices  635 us (35%)
  other arithmetic  297 us (16%)
  matrix products  146 us (8%)
    psum x1, waiting for transfers between devices, on_device(): total = lax.psum(restored, 'dp')  494 us
    gather x2, local copies, waits for them, and re-layouts, on_device(): values = jnp.take_along_axis(coeffs, own, axis=2)  398 us
    unnamed x5, other arithmetic  231 us
    all_to_all x1, waiting for transfers between devices, on_device(): lax.all_to_all(total[None], 'expert', split_axis=2, concat_axis=1, tiled=...  99.3 us
    dot_general x2, matrix products, forward(): jnp.einsum('ui,piqj,vj->pquv', cosine, blocks, cosine, precision=HIGHEST_...  82.3 us
    dot_general x2, matrix products, inverse(): jnp.einsum('ui,pquv,vj->piqj', cosine, coeffs, cosine, precision=HIGHEST_...  63.5 us
    convert_element_type x3, local copies, waits for them, and re-layouts, on_device(): decayed = MOMENTUM_DECAY * momentum.reshape(row_count, col_count) + shift...  53.4 us
    unnamed x26, local copies, waits for them, and re-layouts  48.5 us
  transfers between devices with their start and end apart: 3, of which 3 were waited for; matrix products, arithmetic and copies ran while one was open for 6% of the time, Pallas kernels for 0%

commit v1 on v0

--- a/solution.py
+++ b/solution.py
@@ -51,7 +51,18 @@
     selected = place(values, own, SPAN * SPAN).reshape(block_rows, block_cols, SPAN, SPAN)
     restored = inverse(selected, cosine).reshape(row_count, col_count)
     momentum_next = (decayed - restored).reshape(momentum.shape)
-    total = lax.psum(restored, "dp")
+
+    def loops_prepare(q_in):
+        across = "dp"
+        block_next = q_in
+        num = lax.axis_size(across)
+        for m in [
+            [(src_i, src_i ^ b) for src_i in range(num)] for b in (1, 2, 4, 8, 16) if b < num
+        ]:
+            block_next = block_next + lax.ppermute(block_next, axis_name=across, perm=m)
+        return block_next
+
+    total = loops_prepare(restored)
     update = lax.all_to_all(total[None], "expert", split_axis=2, concat_axis=1, tiled=True)
     return (momentum_next, update)
 

time: 1810 us -> 2270 us (1.25)
  waiting for transfers between devices: 635 us -> 1080 us
    ppermute x0 -> x2, waiting for transfers between devices: none -> 939 us  [loops_prepare(): block_next = block_next + lax.ppermute(block_next, axis_name=across, perm=m)]
    psum x1 -> x0, waiting for transfers between devices: 494 us -> none  [on_device(): total = lax.psum(restored, 'dp')]
    psum x1 -> x0, local copies, waits for them, and re-layouts: 32.1 us -> none  [on_device(): total = lax.psum(restored, 'dp')]
    reshape x1 -> x2, local copies, waits for them, and re-layouts: 25.4 us -> 50.8 us  [on_device(): restored = inverse(selected, cosine).reshape(row_count, col_count)]
  transfers between devices with their start and end apart: 3 -> 4, of which waited for: 3 -> 4; matrix products, arithmetic and copies ran while one was open for 6% -> 5% of each run, Pallas kernels for 0% -> 0%
where the time goes in v1:
time: 2270 us; the launch traced here: 2250 us
  waiting for transfers between devices  1080 us (48%)
  local copies, waits for them, and re-layouts  689 us (30%)
  other arithmetic  310 us (14%)
  matrix products  146 us (6%)
    ppermute x2, waiting for transfers between devices, loops_prepare(): block_next = block_next + lax.ppermute(block_next, axis_name=across, perm=m)  939 us
    gather x2, local copies, waits for them, and re-layouts, on_device(): values = jnp.take_along_axis(coeffs, own, axis=2)  398 us
    unnamed x5, other arithmetic  232 us
    all_to_all x1, waiting for transfers between devices, on_device(): lax.all_to_all(total[None], 'expert', split_axis=2, concat_axis=1, tiled=...  99.5 us
    dot_general x2, matrix products, forward(): jnp.einsum('ui,piqj,vj->pquv', cosine, blocks, cosine, precision=HIGHEST_...  82.3 us
    dot_general x2, matrix products, inverse(): jnp.einsum('ui,pquv,vj->piqj', cosine, coeffs, cosine, precision=HIGHEST_...  63.5 us
    convert_element_type x3, local copies, waits for them, and re-layouts, on_device(): decayed = MOMENTUM_DECAY * momentum.reshape(row_count, col_count) + shift...  53.4 us
    reshape x2, local copies, waits for them, and re-layouts, on_device(): restored = inverse(selected, cosine).reshape(row_count, col_count)  50.8 us
  transfers between devices with their start and end apart: 4, of which 4 were waited for; matrix products, arithmetic and copies ran while one was open for 5% of the time, Pallas kernels for 0%

profile of v1, /device:TPU:0, one launch (start us, length us, event | category | flops | bytes accessed | tf_op | source)
XLA Modules:
  0.0 2245.1 jit_solution(3388913348840540729)
XLA Ops:
  15.1 74.5 %reduce.4 = bf16[14336,256]{1,0:T(8,128)(2,1)} reduce(bf16[14336,1,1,256]{3,2,1,0:T(2,128)(2,1)} %bitcast.52, bf16[]{:T(256)} %broadcast.103), dimensions={1,2}, to_apply=%bitcast.48.reduce_sub_computation | reduce | bytes 14680066
  121.6 24.3 %mul.98 = f32[28,64,32,64]{3,2,1,0:T(8,128)} reshape(f32[1,1,1792,2048]{3,2,1,0:T(8,128)} %broadcast_multiply_fusion) | data formatting | bytes 29360128 | tf_op jit(solution)/shard_map/mul | solution.py:42
  146.2 41.4 %all-to-all-done = bf16[8,2,229376]{2,1,0:T(2,128)(2,1)} async-done(((bf16[8,2,229376]{2,1,0:T(2,128)(2,1)}), bf16[8,2,229376]{2,1,0:T(2,128)(2,1)}, u32[]{:S(2)}, u32[]{:S(2)}) %all-to-all-start) | async-done | bytes 7340064 | tf_op jit(solution)/shard_map/all_to_all | solution.py:39
  199.7 15.9 copy.46
  215.6 21.7 reshape.111
  237.2 29.9 %add.68 = f32[28,64,32,64]{3,2,1,0:T(8,128)} add(f32[28,64,32,64]{3,2,1,0:T(8,128)} %mul.98, f32[28,64,32,64]{3,2,1,0:T(8,128)} %reshape.111) | non-fusion elementwise | flops 3670016 | bytes 44040192 | tf_op jit(solution)/shard_map/add | solution.py:42
  267.1 52.7 %fusion = f32[28,32,64,64]{2,3,1,0:T(8,128)} fusion(f32[28,64,32,64]{3,2,1,0:T(8,128)} %add.68, f32[64]{0:T(128)S(1)} %get-tuple-element.5, f32[64]{0:T(128)S(1)} %get-tuple-element.4), kind=kOutput, calls=%fused_computation.2 | convolution fusion | flops 2818584576 | bytes 29360640 | tf_op jit(solution)/shard_map/ui,piqj,vj->pquv/dot_general | solution.py:20
  319.8 29.7 %fusion.7 = f32[28,32,64,64]{3,2,1,0:T(8,128)} fusion(f32[28,32,64,64]{2,3,1,0:T(8,128)} %fusion, f32[64]{0:T(128)S(1)} %get-tuple-element.5, f32[64]{0:T(128)S(1)} %get-tuple-element.4), kind=kOutput, calls=%fused_computation.22 | convolution fusion | flops 2818584576 | bytes 29360640 | tf_op jit(solution)/shard_map/ui,piqj,vj->pquv/dot_general | solution.py:20
  349.5 24.7 %reshape.101 = f32[28,32,4096]{2,1,0:T(8,128)} reshape(f32[28,32,64,64]{3,2,1,0:T(8,128)} %fusion.7) | data formatting | bytes 29360128 | tf_op jit(solution)/shard_map/reshape | solution.py:48
  374.2 398.1 %gather_fusion = f32[28672]{0:T(1024)S(1)} fusion(f32[28,32,4096]{2,1,0:T(8,128)} %reshape.101, s32[28672]{0:T(1024)S(1)} %reshape.114), kind=kCustom, calls=%fused_computation | custom fusion | bytes 573440 | tf_op jit(solution)/shard_map/jit(take_along_axis)/gather | solution.py:50
  772.8 156.3 %scatter_custom_fusion = f32[3670016]{0:T(1024)} fusion(s32[28672]{0:T(1024)} %reshape.120, f32[28672]{0:T(1024)S(1)} %reshape.122, f32[]{:T(128)} %constant.15.clone.1), kind=kCustom, calls=%fused_computation.8 | custom fusion | flops 28672 | bytes 14680576
  929.1 22.2 reshape.102
  951.3 34.3 %fusion.5 = f32[28,32,64,64]{2,3,1,0:T(8,128)} fusion(f32[28,32,64,64]{3,2,1,0:T(8,128)} %reshape.102, f32[64]{0:T(128)S(1)} %copy-done.7, f32[64]{0:T(128)S(1)} %copy-done.5), kind=kOutput, calls=%fused_computation.20 | convolution fusion | flops 2818584576 | bytes 29360640 | tf_op jit(solution)/shard_map/ui,pquv,vj->piqj/dot_general | solution.py:24
  985.6 29.2 %convolution_bitcast_fusion = f32[28,64,32,64]{3,1,2,0:T(8,128)S(1)} fusion(f32[28,32,64,64]{2,3,1,0:T(8,128)} %fusion.5, f32[64]{0:T(128)S(1)} %copy-done.7, f32[64]{0:T(128)S(1)} %copy-done.5), kind=kOutput, calls=%fused_computation.7 | convolution fusion | flops 2818584576 | bytes 29360640 | tf_op jit(solution)/shard_map/ui,pquv,vj->piqj/dot_general | solution.py:24
  1014.8 19.3 copy.33
  1034.1 25.4 %reshape.104 = f32[1792,2048]{1,0:T(8,128)} reshape(f32[28,64,32,64]{3,2,1,0:T(8,128)} %copy.33) | data formatting | bytes 29360128 | tf_op jit(solution)/shard_map/reshape | solution.py:52
  1062.2 312.7 %collective-permute-done = f32[1792,2048]{1,0:T(8,128)S(1)} collective-permute-done((f32[1792,2048]{1,0:T(8,128)}, f32[1792,2048]{1,0:T(8,128)S(1)}, u32[]{:S(2)}, u32[]{:S(2)}) %collective-permute-start) | collective-permute-done | bytes 14680096 | tf_op jit(solution)/shard_map/ppermute | solution.py:62
  1384.8 626.6 %collective-permute-done.1 = f32[1792,2048]{1,0:T(8,128)S(1)} collective-permute-done((f32[1792,2048]{1,0:T(8,128)S(1)}, f32[1792,2048]{1,0:T(8,128)S(1)}, u32[]{:S(2)}, u32[]{:S(2)}) %collective-permute-start.1) | collective-permute-done | bytes 14680096 | tf_op jit(solution)/shard_map/ppermute | solution.py:62
  2017.9 32.0 %copy.35 = f32[1,1792,2048]{1,0,2:T(1,128)} copy(f32[1,1792,2048]{2,1,0:T(8,128)} %add_bitcast_fusion) | data formatting | bytes 29360128 | tf_op jit(solution)/shard_map/broadcast_in_dim | solution.py:66
  2057.5 25.4 %reshape.103 = f32[1,1,1792,2048]{3,2,1,0:T(8,128)} reshape(f32[28,64,32,64]{3,2,1,0:T(8,128)} %copy.33) | data formatting | bytes 29360128 | tf_op jit(solution)/shard_map/reshape | solution.py:52
  2082.9 15.8 reshape.110
  2098.7 20.9 add_subtract_fusion
  2119.7 99.5 %all-to-all-done.1 = f32[1,1792,2048]{1,0,2:T(1,128)} async-done(((f32[1,1792,2048]{1,0,2:T(1,128)}), f32[1,1792,2048]{1,0,2:T(1,128)}, u32[]{:S(2)}, u32[]{:S(2)}) %all-to-all-start.1) | async-done | bytes 14680096 | tf_op jit(solution)/shard_map/all_to_all | solution.py:66
  2230.5 14.4 copy.36
  (45 shorter events, 97.1 us)
Async XLA Ops:
  0.6 103.8 %copy-start = (s32[28,32,4,32]{3,2,1,0:T(4,128)S(1)}, s32[28,32,4,32]{3,2,1,0:T(4,128)}, u32[]{:S(2)}) copy-start(s32[28,32,4,32]{3,2,1,0:T(4,128)} %param.5) | copy-start | bytes 1376260
  89.6 16.4 copy-start.9
  89.6 16.7 copy-start.8
  98.7 88.9 %all-to-all-start = ((bf16[8,2,229376]{2,1,0:T(2,128)(2,1)}), bf16[8,2,229376]{2,1,0:T(2,128)(2,1)}, u32[]{:S(2)}, u32[]{:S(2)}) async-start(bf16[8,2,229376]{2,1,0:T(2,128)(2,1)} %reshape.129), calls=%async_computation | async-start | bytes 14680064 | tf_op jit(solution)/shard_map/all_to_all | solution.py:39
  105.0 0.8 copy-start.2
  146.1 173.7 %copy-start.4 = (f32[64]{0:T(128)}, f32[64]{0:T(128)S(1)}, u32[]{:S(2)}) copy-start(f32[64]{0:T(128)S(1)} %get-tuple-element.4) | copy-start | bytes 772
  146.1 173.7 %copy-start.6 = (f32[64]{0:T(128)}, f32[64]{0:T(128)S(1)}, u32[]{:S(2)}) copy-start(f32[64]{0:T(128)S(1)} %get-tuple-element.5) | copy-start | bytes 772
  374.2 398.3 %copy-start.3 = (s32[28,32,1,32]{3,2,1,0:T(1,128)S(1)}, s32[28,32,1,32]{3,2,1,0:T(1,128)}, u32[]{:S(2)}) copy-start(s32[28,32,1,32]{3,2,1,0:T(1,128)} %copy-done.2) | copy-start | bytes 344068
  929.1 22.2 copy-start.5
  929.1 22.2 copy-start.7
  1059.5 315.4 %collective-permute-start = (f32[1792,2048]{1,0:T(8,128)}, f32[1792,2048]{1,0:T(8,128)S(1)}, u32[]{:S(2)}, u32[]{:S(2)}) collective-permute-start(f32[1792,2048]{1,0:T(8,128)} %reshape.104), channel_id=1, source_target_pairs={{0,1},{1,0},{2,3},{3,2},{4,5},{5,4},{6,7},{7,6},{8,9},{9,8},{10,11... | collective-permute-start | bytes 44040200 | tf_op jit(solution)/shard_map/ppermute | solution.py:62
  1381.9 629.6 %collective-permute-start.1 = (f32[1792,2048]{1,0:T(8,128)S(1)}, f32[1792,2048]{1,0:T(8,128)S(1)}, u32[]{:S(2)}, u32[]{:S(2)}) collective-permute-start(f32[1792,2048]{1,0:T(8,128)S(1)} %add.71), channel_id=1, source_target_pairs={{0,2},{1,3},{2,0},{3,1},{4,6},{5,7},{6,4},{7,5},{8,10},{9,11},{10,... | collective-permute-start | bytes 44040200 | tf_op jit(solution)/shard_map/ppermute | solution.py:62
  2049.9 169.3 %all-to-all-start.1 = ((f32[1,1792,2048]{1,0,2:T(1,128)}), f32[1,1792,2048]{1,0,2:T(1,128)}, u32[]{:S(2)}, u32[]{:S(2)}) async-start(f32[1,1792,2048]{1,0,2:T(1,128)} %copy.35), calls=%async_computation.1 | async-start | bytes 29360128 | tf_op jit(solution)/shard_map/all_to_all | solution.py:66
  2230.5 14.4 copy-start.1
